TPU v7x, 256 devices: a whole 4x4x8 slice. The times are simulated.
256 devices in a mesh: section: 16 (over x, y), tensor: 16 (over z, core).
Axes of the slice: x: 4, y: 4, z: 8, core: 2. Of those that a mesh axis runs over, the one named last changes fastest.
Arguments:
- token_ids: int32 [3, 48], replicated, may hold values from 0 to 31999
- emb_table: bfloat16 [32000, 4096], P('section', 'tensor'), may hold values from -6 to 6
- attn_gain: bfloat16 [16, 4096], P('section'), may hold values from 0.25 to 1.75
- query_weight: bfloat16 [16, 4096, 4096], P('section', None, 'tensor'), may hold values from -8 to 8
- key_weight: bfloat16 [16, 4096, 4096], P('section', None, 'tensor'), may hold values from -8 to 8
- value_weight: bfloat16 [16, 4096, 4096], P('section', None, 'tensor'), may hold values from -0.09375 to 0.09375
- mix_weight: float32 [16, 32], P('section', 'tensor'), may hold values from 0.2 to 0.8
- out_weight: bfloat16 [16, 4096, 4096], P('section', 'tensor'), may hold values from -0.125 to 0.125
Outputs:
- layer_outputs: bfloat16 [16, 3, 48, 4096], P('section', None, None, 'tensor')
All inputs are finite; a program needn't handle non-finite values.
Results may differ from a plain program's by a relative error of at most 0.033.
Values may be sent and summed in bfloat16 or wider, within the bound.
A program may use at most 64 MiB of HBM per device.

v0:
```python
import jax
import jax.numpy as jnp
from jax import lax
from jax.sharding import PartitionSpec as P

EPSILON = 1e-05
ROTARY_BASE = 10000.0


def from_everyone(array, axis):
    peers = lax.axis_size(axis)
    return lax.all_to_all(
        jnp.broadcast_to(array[None], (peers, *array.shape)), axis, 0, 0, tiled=True
    )


def of_everyone(array, axis):
    return from_everyone(array, axis).astype(jnp.float32).sum(axis=0)


def broadcast(array, axis, root):
    return lax.dynamic_index_in_dim(lax.all_gather(array, axis), root, 0, keepdims=False)


def laid_out(pieces, dim):
    lengths = list(pieces.shape[1:])
    lengths[dim] *= pieces.shape[0]
    return jnp.moveaxis(pieces, 0, dim).reshape(lengths)


def gather_directly(array, axis, dim):
    return laid_out(from_everyone(array, axis), dim)


def in_blocks(array, dim, peers):
    lengths = array.shape
    pieces = array.reshape(*lengths[:dim], peers, lengths[dim] // peers, *lengths[dim + 1 :])
    return jnp.moveaxis(pieces, dim, 0)


def summed_on_arrival(array, axis, dim):
    pieces = in_blocks(array, dim, lax.axis_size(axis))
    arrived = lax.all_to_all(pieces, axis, split_axis=0, concat_axis=0, tiled=True)
    return arrived.astype(jnp.float32).sum(axis=0)


def shifted(value, axis, steps):
    count = lax.axis_size(axis)
    first, last = (max(0, -steps), min(count, count - steps))
    return lax.ppermute(value, axis, [(source, source + steps) for source in range(first, last)])


def rms_scale(values, norm_gain):
    mean_square = jnp.mean(values * values, axis=-1, keepdims=True)
    return values * lax.rsqrt(mean_square + EPSILON) * norm_gain


def rotate(values):
    length = values.shape[-3]
    head_dim = values.shape[-1]
    half_dim = head_dim // 2
    positions = jnp.arange(length, dtype=jnp.float32)
    frequency = ROTARY_BASE ** (-(jnp.arange(half_dim, dtype=jnp.float32) * 2.0) / head_dim)
    angles = positions[:, None] * frequency[None, :]
    cosine = jnp.cos(angles)[:, None, :]
    sine_table = jnp.sin(angles)[:, None, :]
    leading = values[..., :half_dim]
    second = values[..., half_dim:]
    return jnp.concatenate(
        [leading * cosine - second * sine_table, second * cosine + leading * sine_table], axis=-1
    )


def attend(queries, key_rows, mixed_values):
    length = queries.shape[0]
    head_dim = queries.shape[2]
    scores = jnp.einsum(
        "qhd,khd->hqk", queries, key_rows, preferred_element_type=jnp.float32
    ) * head_dim ** (-0.5)
    causal = jnp.arange(length)[:, None] >= jnp.arange(length)[None, :]
    scores = jnp.where(causal, scores, -1e30)
    row_top = jnp.max(scores, axis=-1, keepdims=True)
    expo = jnp.exp(scores - row_top)
    attn_probs = (expo / jnp.sum(expo, axis=-1, keepdims=True)).astype(jnp.bfloat16)
    attended = jnp.einsum(
        "hqk,khd->qhd", attn_probs, mixed_values, preferred_element_type=jnp.float32
    )
    return attended.astype(jnp.bfloat16)


def shards(
    token_ids, emb_table, attn_gain, query_weight, key_weight, value_weight, mix_weight, out_weight
):
    section_rank = lax.axis_index("section")
    section_count = lax.axis_size("section")
    batches, length = token_ids.shape
    vocab_local, width_local = emb_table.shape
    head_local = mix_weight.shape[1]
    head_dim = query_weight.shape[2] // head_local
    norm_gain = attn_gain[0].astype(jnp.float32)
    w_query = query_weight[0]
    w_key = key_weight[0]
    w_value = value_weight[0]
    w_out = out_weight[0]
    mix_rate = mix_weight[0][None, :, None]
    flat_ids = token_ids.reshape(-1) - section_rank * vocab_local
    one_hot = (flat_ids[:, None] == jnp.arange(vocab_local, dtype=jnp.int32)[None, :]).astype(
        jnp.bfloat16
    )
    looked = jnp.dot(one_hot, emb_table, preferred_element_type=jnp.float32)
    first_shard = (
        of_everyone(looked.astype(jnp.bfloat16), "section").astype(jnp.float32).astype(jnp.bfloat16)
    )
    first_full = lax.all_gather(first_shard, "tensor", axis=1, tiled=True)
    first_float = first_full.astype(jnp.float32)

    def root_project():
        first_norm = rms_scale(first_float, norm_gain).astype(jnp.bfloat16)
        return jnp.dot(first_norm, w_value, preferred_element_type=jnp.float32).astype(jnp.bfloat16)

    def skipped():
        return jnp.zeros((first_full.shape[0], w_value.shape[1]), jnp.bfloat16)

    own_values = lax.cond(section_rank == 0, root_project, skipped)
    first_values = broadcast(own_values, "section", 0)
    source_values = first_values.reshape(batches, length, head_local, head_dim)
    first_blocks = first_shard.reshape(batches, length, width_local)

    def attention_branch(full_rows, micro_index):
        normed = rms_scale(full_rows.astype(jnp.float32), norm_gain).astype(jnp.bfloat16)
        queries = jnp.dot(normed, w_query, preferred_element_type=jnp.float32)
        key_rows = jnp.dot(normed, w_key, preferred_element_type=jnp.float32)
        values = jnp.dot(normed, w_value, preferred_element_type=jnp.float32)
        queries = rotate(queries.reshape(length, head_local, head_dim)).astype(jnp.bfloat16)
        key_rows = rotate(key_rows.reshape(length, head_local, head_dim)).astype(jnp.bfloat16)
        values = values.reshape(length, head_local, head_dim)
        picked = lax.dynamic_index_in_dim(source_values, micro_index, 0, keepdims=False).astype(
            jnp.float32
        )
        mixed_values = (mix_rate * values + (1.0 - mix_rate) * picked).astype(jnp.bfloat16)
        attended = attend(queries, key_rows, mixed_values).reshape(length, head_local * head_dim)
        return jnp.dot(attended, w_out, preferred_element_type=jnp.float32)

    def advance(step_index, loop_state):
        incoming, outputs = loop_state
        position = step_index - section_rank
        is_valid = (position >= 0) & (position < batches)
        micro_index = jnp.clip(position, 0, batches - 1)
        starting = lax.dynamic_index_in_dim(first_blocks, micro_index, 0, keepdims=False)
        shard_rows = jnp.where(section_rank == 0, starting, incoming)
        full_rows = gather_directly(shard_rows, "tensor", 1)
        summed = summed_on_arrival(
            attention_branch(full_rows, micro_index).astype(jnp.bfloat16), "tensor", 1
        )
        fresh_rows = (shard_rows.astype(jnp.float32) + summed).astype(jnp.bfloat16)
        previous = lax.dynamic_index_in_dim(outputs, micro_index, 0, keepdims=False)
        kept_rows = jnp.where(is_valid, fresh_rows, previous)
        outputs = lax.dynamic_update_index_in_dim(outputs, kept_rows, micro_index, 0)
        incoming = shifted(fresh_rows, "section", 1)
        return (incoming, outputs)

    incoming = jnp.zeros((length, width_local), jnp.bfloat16)
    outputs = jnp.zeros((batches, length, width_local), jnp.bfloat16)
    step_count = batches + section_count - 1
    incoming, outputs = lax.fori_loop(0, step_count, advance, (incoming, outputs))
    return outputs[None]


def solution(mesh):
    in_specs = (
        P(),
        P("section", "tensor"),
        P("section", None),
        P("section", None, "tensor"),
        P("section", None, "tensor"),
        P("section", None, "tensor"),
        P("section", "tensor"),
        P("section", "tensor", None),
    )
    out_specs = P("section", None, None, "tensor")
    return jax.shard_map(shards, mesh=mesh, in_specs=in_specs, out_specs=out_specs, check_vma=False)
```

profile of v0, /device:TPU:31, one launch (start us, length us, event | category | flops | bytes accessed | tf_op | source)
XLA Modules:
  0.0 1193.7 jit_solution(4408953827602636049)
XLA Ops:
  8.2 20.8 %all_to_all.29 = bf16[16,144,256]{2,1,0:T(8,128)(2,1)} all-to-all(bf16[16,144,256]{2,1,0:T(8,128)(2,1)S(1)} %broadcast_in_dim.99), channel_id=1, replica_groups=mesh['section'=16,'tensor'=16] {'section'}, dimensions={0} | all-to-all | bytes 2359296 | tf_op jit(solution)/shard_map/all_to_all | solution.py:12
  34.1 39.0 %all-gather.4.cloned.1.call-done = bf16[144,4096]{1,0:T(8,128)(2,1)} async-done(((bf16[144,256]{1,0:T(8,128)(2,1)}), bf16[144,4096]{1,0:T(8,128)(2,1)}) %all-gather.4.cloned.1.call-update) | async-done | bytes 1179664 | tf_op jit(solution)/shard_map/all_gather | solution.py:114
  85.1 34.9 %all-gather.6.cloned.1.call-done = bf16[2304,256]{1,0:T(8,128)(2,1)} async-done(((bf16[144,256]{1,0:T(8,128)(2,1)}), bf16[2304,256]{1,0:T(8,128)(2,1)}) %all-gather.6.cloned.1.call-update) | async-done | bytes 1179664 | tf_op jit(solution)/shard_map/all_gather | solution.py:22
  122.2 1064.7 %while.17 = (s32[]{:T(128)}, bf16[48,256]{1,0:T(8,128)(2,1)S(1)}, bf16[3,48,256]{2,1,0:T(8,128)(2,1)}, pred[]{:T(512)}, s32[]{:T(128)}, /*index=5*/bf16[3,48,256...) while((s32[]{:T(128)}, bf16[48,256]{1,0:T(8,128)(2,1)S(1)}, ...), condition=%wide.wide.region_9.10_spmd, body=%wide.wide.region_4.9_spmd.sunk | while | flops 407331392 | bytes 26102732 | solution.py:165
  123.7 9.0 all-to-all-start
  136.6 10.5 all-to-all-done
  165.8 12.5 %all-to-all-done.1 = bf16[16,48,256]{2,1,0:T(8,128)(2,1)S(1)} async-done(((bf16[16,48,256]{2,1,0:T(8,128)(2,1)}), bf16[16,48,256]{2,1,0:T(8,128)(2,1)S(1)}, u32[]{:S(2)}, u32[]{:S(2)}) %all-to-all-start.1) | async-done | bytes 393248 | tf_op jit(solution)/shard_map/while/body/eval_jaxpr/all_to_all | solution.py:43
  193.9 10.5 all-to-all-done
  223.0 12.5 %all-to-all-done.1 = bf16[16,48,256]{2,1,0:T(8,128)(2,1)S(1)} async-done(((bf16[16,48,256]{2,1,0:T(8,128)(2,1)}), bf16[16,48,256]{2,1,0:T(8,128)(2,1)S(1)}, u32[]{:S(2)}, u32[]{:S(2)}) %all-to-all-start.1) | async-done | bytes 393248 | tf_op jit(solution)/shard_map/while/body/eval_jaxpr/all_to_all | solution.py:43
  251.1 10.5 all-to-all-done
  280.3 12.5 %all-to-all-done.1 = bf16[16,48,256]{2,1,0:T(8,128)(2,1)S(1)} async-done(((bf16[16,48,256]{2,1,0:T(8,128)(2,1)}), bf16[16,48,256]{2,1,0:T(8,128)(2,1)S(1)}, u32[]{:S(2)}, u32[]{:S(2)}) %all-to-all-start.1) | async-done | bytes 393248 | tf_op jit(solution)/shard_map/while/body/eval_jaxpr/all_to_all | solution.py:43
  308.3 10.5 all-to-all-done
  337.5 12.5 %all-to-all-done.1 = bf16[16,48,256]{2,1,0:T(8,128)(2,1)S(1)} async-done(((bf16[16,48,256]{2,1,0:T(8,128)(2,1)}), bf16[16,48,256]{2,1,0:T(8,128)(2,1)S(1)}, u32[]{:S(2)}, u32[]{:S(2)}) %all-to-all-start.1) | async-done | bytes 393248 | tf_op jit(solution)/shard_map/while/body/eval_jaxpr/all_to_all | solution.py:43
  365.5 10.5 all-to-all-done
  394.7 12.5 %all-to-all-done.1 = bf16[16,48,256]{2,1,0:T(8,128)(2,1)S(1)} async-done(((bf16[16,48,256]{2,1,0:T(8,128)(2,1)}), bf16[16,48,256]{2,1,0:T(8,128)(2,1)S(1)}, u32[]{:S(2)}, u32[]{:S(2)}) %all-to-all-start.1) | async-done | bytes 393248 | tf_op jit(solution)/shard_map/while/body/eval_jaxpr/all_to_all | solution.py:43
  424.8 10.5 all-to-all-done
  453.9 12.5 %all-to-all-done.1 = bf16[16,48,256]{2,1,0:T(8,128)(2,1)S(1)} async-done(((bf16[16,48,256]{2,1,0:T(8,128)(2,1)}), bf16[16,48,256]{2,1,0:T(8,128)(2,1)S(1)}, u32[]{:S(2)}, u32[]{:S(2)}) %all-to-all-start.1) | async-done | bytes 393248 | tf_op jit(solution)/shard_map/while/body/eval_jaxpr/all_to_all | solution.py:43
  469.2 5.7 collective-permute-done
  484.1 10.5 all-to-all-done
  513.3 12.5 %all-to-all-done.1 = bf16[16,48,256]{2,1,0:T(8,128)(2,1)S(1)} async-done(((bf16[16,48,256]{2,1,0:T(8,128)(2,1)}), bf16[16,48,256]{2,1,0:T(8,128)(2,1)S(1)}, u32[]{:S(2)}, u32[]{:S(2)}) %all-to-all-start.1) | async-done | bytes 393248 | tf_op jit(solution)/shard_map/while/body/eval_jaxpr/all_to_all | solution.py:43
  528.5 5.7 collective-permute-done
  543.4 10.5 all-to-all-done
  572.6 12.5 %all-to-all-done.1 = bf16[16,48,256]{2,1,0:T(8,128)(2,1)S(1)} async-done(((bf16[16,48,256]{2,1,0:T(8,128)(2,1)}), bf16[16,48,256]{2,1,0:T(8,128)(2,1)S(1)}, u32[]{:S(2)}, u32[]{:S(2)}) %all-to-all-start.1) | async-done | bytes 393248 | tf_op jit(solution)/shard_map/while/body/eval_jaxpr/all_to_all | solution.py:43
  602.8 10.5 all-to-all-done
  631.9 12.5 %all-to-all-done.1 = bf16[16,48,256]{2,1,0:T(8,128)(2,1)S(1)} async-done(((bf16[16,48,256]{2,1,0:T(8,128)(2,1)}), bf16[16,48,256]{2,1,0:T(8,128)(2,1)S(1)}, u32[]{:S(2)}, u32[]{:S(2)}) %all-to-all-start.1) | async-done | bytes 393248 | tf_op jit(solution)/shard_map/while/body/eval_jaxpr/all_to_all | solution.py:43
  647.2 5.7 collective-permute-done
  662.1 10.5 all-to-all-done
  691.3 12.5 %all-to-all-done.1 = bf16[16,48,256]{2,1,0:T(8,128)(2,1)S(1)} async-done(((bf16[16,48,256]{2,1,0:T(8,128)(2,1)}), bf16[16,48,256]{2,1,0:T(8,128)(2,1)S(1)}, u32[]{:S(2)}, u32[]{:S(2)}) %all-to-all-start.1) | async-done | bytes 393248 | tf_op jit(solution)/shard_map/while/body/eval_jaxpr/all_to_all | solution.py:43
  706.5 5.7 collective-permute-done
  721.4 10.5 all-to-all-done
  750.6 12.5 %all-to-all-done.1 = bf16[16,48,256]{2,1,0:T(8,128)(2,1)S(1)} async-done(((bf16[16,48,256]{2,1,0:T(8,128)(2,1)}), bf16[16,48,256]{2,1,0:T(8,128)(2,1)S(1)}, u32[]{:S(2)}, u32[]{:S(2)}) %all-to-all-start.1) | async-done | bytes 393248 | tf_op jit(solution)/shard_map/while/body/eval_jaxpr/all_to_all | solution.py:43
  780.8 10.5 all-to-all-done
  809.9 12.5 %all-to-all-done.1 = bf16[16,48,256]{2,1,0:T(8,128)(2,1)S(1)} async-done(((bf16[16,48,256]{2,1,0:T(8,128)(2,1)}), bf16[16,48,256]{2,1,0:T(8,128)(2,1)S(1)}, u32[]{:S(2)}, u32[]{:S(2)}) %all-to-all-start.1) | async-done | bytes 393248 | tf_op jit(solution)/shard_map/while/body/eval_jaxpr/all_to_all | solution.py:43
  840.1 10.5 all-to-all-done
  869.3 12.5 %all-to-all-done.1 = bf16[16,48,256]{2,1,0:T(8,128)(2,1)S(1)} async-done(((bf16[16,48,256]{2,1,0:T(8,128)(2,1)}), bf16[16,48,256]{2,1,0:T(8,128)(2,1)S(1)}, u32[]{:S(2)}, u32[]{:S(2)}) %all-to-all-start.1) | async-done | bytes 393248 | tf_op jit(solution)/shard_map/while/body/eval_jaxpr/all_to_all | solution.py:43
  899.4 10.5 all-to-all-done
  928.6 12.5 %all-to-all-done.1 = bf16[16,48,256]{2,1,0:T(8,128)(2,1)S(1)} async-done(((bf16[16,48,256]{2,1,0:T(8,128)(2,1)}), bf16[16,48,256]{2,1,0:T(8,128)(2,1)S(1)}, u32[]{:S(2)}, u32[]{:S(2)}) %all-to-all-start.1) | async-done | bytes 393248 | tf_op jit(solution)/shard_map/while/body/eval_jaxpr/all_to_all | solution.py:43
  958.8 10.5 all-to-all-done
  987.9 12.5 %all-to-all-done.1 = bf16[16,48,256]{2,1,0:T(8,128)(2,1)S(1)} async-done(((bf16[16,48,256]{2,1,0:T(8,128)(2,1)}), bf16[16,48,256]{2,1,0:T(8,128)(2,1)S(1)}, u32[]{:S(2)}, u32[]{:S(2)}) %all-to-all-start.1) | async-done | bytes 393248 | tf_op jit(solution)/shard_map/while/body/eval_jaxpr/all_to_all | solution.py:43
  1003.2 5.7 collective-permute-done
  1018.1 10.5 all-to-all-done
  1047.3 12.5 %all-to-all-done.1 = bf16[16,48,256]{2,1,0:T(8,128)(2,1)S(1)} async-done(((bf16[16,48,256]{2,1,0:T(8,128)(2,1)}), bf16[16,48,256]{2,1,0:T(8,128)(2,1)S(1)}, u32[]{:S(2)}, u32[]{:S(2)}) %all-to-all-start.1) | async-done | bytes 393248 | tf_op jit(solution)/shard_map/while/body/eval_jaxpr/all_to_all | solution.py:43
  1062.5 5.7 collective-permute-done
  1077.4 10.5 all-to-all-done
  1106.6 12.5 %all-to-all-done.1 = bf16[16,48,256]{2,1,0:T(8,128)(2,1)S(1)} async-done(((bf16[16,48,256]{2,1,0:T(8,128)(2,1)}), bf16[16,48,256]{2,1,0:T(8,128)(2,1)S(1)}, u32[]{:S(2)}, u32[]{:S(2)}) %all-to-all-start.1) | async-done | bytes 393248 | tf_op jit(solution)/shard_map/while/body/eval_jaxpr/all_to_all | solution.py:43
  1121.9 5.7 collective-permute-done
  1136.8 10.5 all-to-all-done
  1165.9 12.5 %all-to-all-done.1 = bf16[16,48,256]{2,1,0:T(8,128)(2,1)S(1)} async-done(((bf16[16,48,256]{2,1,0:T(8,128)(2,1)}), bf16[16,48,256]{2,1,0:T(8,128)(2,1)S(1)}, u32[]{:S(2)}, u32[]{:S(2)}) %all-to-all-start.1) | async-done | bytes 393248 | tf_op jit(solution)/shard_map/while/body/eval_jaxpr/all_to_all | solution.py:43
  (597 shorter events, 619.2 us)
Async XLA Ops:
  6.5 66.7 %all-gather.4.cloned.1.call-start = ((), (), s32[]{:S(2)}) async-start(), calls=%async_computation.3 | async-start | bytes 1253376 | tf_op jit(solution)/shard_map/all_gather | solution.py:114
  31.1 88.8 %all-gather.6.cloned.1.call-start = ((), (), s32[]{:S(2)}) async-start(), calls=%async_computation.4 | async-start | bytes 1253376 | tf_op jit(solution)/shard_map/all_gather | solution.py:22
  123.7 23.5 %all-to-all-start = ((bf16[16,48,256]{2,1,0:T(8,128)(2,1)}), bf16[16,48,256]{2,1,0:T(8,128)(2,1)S(1)}, u32[]{:S(2)}, u32[]{:S(2)}) async-start(bf16[16,48,256]{2,1,0:T(8,128)(2,1)} %broadcast_in_dim.123), calls=%async_computation | async-start | bytes 786432 | tf_op jit(solution)/shard_map/while/body/eval_jaxpr/all_to_all | solution.py:12
  161.0 17.4 %all-to-all-start.1 = ((bf16[16,48,256]{2,1,0:T(8,128)(2,1)}), bf16[16,48,256]{2,1,0:T(8,128)(2,1)S(1)}, u32[]{:S(2)}, u32[]{:S(2)}) async-start(bf16[16,48,256]{2,1,0:T(8,128)(2,1)} %bitcast.132), calls=%async_computation.1 | async-start | bytes 786432 | tf_op jit(solution)/shard_map/while/body/eval_jaxpr/all_to_all | solution.py:43
  186.1 18.3 %all-to-all-start = ((bf16[16,48,256]{2,1,0:T(8,128)(2,1)}), bf16[16,48,256]{2,1,0:T(8,128)(2,1)S(1)}, u32[]{:S(2)}, u32[]{:S(2)}) async-start(bf16[16,48,256]{2,1,0:T(8,128)(2,1)} %broadcast_in_dim.123), calls=%async_computation | async-start | bytes 786432 | tf_op jit(solution)/shard_map/while/body/eval_jaxpr/all_to_all | solution.py:12
  218.2 17.4 %all-to-all-start.1 = ((bf16[16,48,256]{2,1,0:T(8,128)(2,1)}), bf16[16,48,256]{2,1,0:T(8,128)(2,1)S(1)}, u32[]{:S(2)}, u32[]{:S(2)}) async-start(bf16[16,48,256]{2,1,0:T(8,128)(2,1)} %bitcast.132), calls=%async_computation.1 | async-start | bytes 786432 | tf_op jit(solution)/shard_map/while/body/eval_jaxpr/all_to_all | solution.py:43
  243.3 18.3 %all-to-all-start = ((bf16[16,48,256]{2,1,0:T(8,128)(2,1)}), bf16[16,48,256]{2,1,0:T(8,128)(2,1)S(1)}, u32[]{:S(2)}, u32[]{:S(2)}) async-start(bf16[16,48,256]{2,1,0:T(8,128)(2,1)} %broadcast_in_dim.123), calls=%async_computation | async-start | bytes 786432 | tf_op jit(solution)/shard_map/while/body/eval_jaxpr/all_to_all | solution.py:12
  275.4 17.4 %all-to-all-start.1 = ((bf16[16,48,256]{2,1,0:T(8,128)(2,1)}), bf16[16,48,256]{2,1,0:T(8,128)(2,1)S(1)}, u32[]{:S(2)}, u32[]{:S(2)}) async-start(bf16[16,48,256]{2,1,0:T(8,128)(2,1)} %bitcast.132), calls=%async_computation.1 | async-start | bytes 786432 | tf_op jit(solution)/shard_map/while/body/eval_jaxpr/all_to_all | solution.py:43
  300.5 18.3 %all-to-all-start = ((bf16[16,48,256]{2,1,0:T(8,128)(2,1)}), bf16[16,48,256]{2,1,0:T(8,128)(2,1)S(1)}, u32[]{:S(2)}, u32[]{:S(2)}) async-start(bf16[16,48,256]{2,1,0:T(8,128)(2,1)} %broadcast_in_dim.123), calls=%async_computation | async-start | bytes 786432 | tf_op jit(solution)/shard_map/while/body/eval_jaxpr/all_to_all | solution.py:12
  332.7 17.4 %all-to-all-start.1 = ((bf16[16,48,256]{2,1,0:T(8,128)(2,1)}), bf16[16,48,256]{2,1,0:T(8,128)(2,1)S(1)}, u32[]{:S(2)}, u32[]{:S(2)}) async-start(bf16[16,48,256]{2,1,0:T(8,128)(2,1)} %bitcast.132), calls=%async_computation.1 | async-start | bytes 786432 | tf_op jit(solution)/shard_map/while/body/eval_jaxpr/all_to_all | solution.py:43
  357.7 18.4 %all-to-all-start = ((bf16[16,48,256]{2,1,0:T(8,128)(2,1)}), bf16[16,48,256]{2,1,0:T(8,128)(2,1)S(1)}, u32[]{:S(2)}, u32[]{:S(2)}) async-start(bf16[16,48,256]{2,1,0:T(8,128)(2,1)} %broadcast_in_dim.123), calls=%async_computation | async-start | bytes 786432 | tf_op jit(solution)/shard_map/while/body/eval_jaxpr/all_to_all | solution.py:12
  389.9 17.4 %all-to-all-start.1 = ((bf16[16,48,256]{2,1,0:T(8,128)(2,1)}), bf16[16,48,256]{2,1,0:T(8,128)(2,1)S(1)}, u32[]{:S(2)}, u32[]{:S(2)}) async-start(bf16[16,48,256]{2,1,0:T(8,128)(2,1)} %bitcast.132), calls=%async_computation.1 | async-start | bytes 786432 | tf_op jit(solution)/shard_map/while/body/eval_jaxpr/all_to_all | solution.py:43
  417.0 18.3 %all-to-all-start = ((bf16[16,48,256]{2,1,0:T(8,128)(2,1)}), bf16[16,48,256]{2,1,0:T(8,128)(2,1)S(1)}, u32[]{:S(2)}, u32[]{:S(2)}) async-start(bf16[16,48,256]{2,1,0:T(8,128)(2,1)} %broadcast_in_dim.123), calls=%async_computation | async-start | bytes 786432 | tf_op jit(solution)/shard_map/while/body/eval_jaxpr/all_to_all | solution.py:12
  449.1 17.4 %all-to-all-start.1 = ((bf16[16,48,256]{2,1,0:T(8,128)(2,1)}), bf16[16,48,256]{2,1,0:T(8,128)(2,1)S(1)}, u32[]{:S(2)}, u32[]{:S(2)}) async-start(bf16[16,48,256]{2,1,0:T(8,128)(2,1)} %bitcast.132), calls=%async_computation.1 | async-start | bytes 786432 | tf_op jit(solution)/shard_map/while/body/eval_jaxpr/all_to_all | solution.py:43
  467.9 7.0 collective-permute-start
  476.4 18.3 %all-to-all-start = ((bf16[16,48,256]{2,1,0:T(8,128)(2,1)}), bf16[16,48,256]{2,1,0:T(8,128)(2,1)S(1)}, u32[]{:S(2)}, u32[]{:S(2)}) async-start(bf16[16,48,256]{2,1,0:T(8,128)(2,1)} %broadcast_in_dim.123), calls=%async_computation | async-start | bytes 786432 | tf_op jit(solution)/shard_map/while/body/eval_jaxpr/all_to_all | solution.py:12
  508.4 17.4 %all-to-all-start.1 = ((bf16[16,48,256]{2,1,0:T(8,128)(2,1)}), bf16[16,48,256]{2,1,0:T(8,128)(2,1)S(1)}, u32[]{:S(2)}, u32[]{:S(2)}) async-start(bf16[16,48,256]{2,1,0:T(8,128)(2,1)} %bitcast.132), calls=%async_computation.1 | async-start | bytes 786432 | tf_op jit(solution)/shard_map/while/body/eval_jaxpr/all_to_all | solution.py:43
  527.2 7.0 collective-permute-start
  535.7 18.3 %all-to-all-start = ((bf16[16,48,256]{2,1,0:T(8,128)(2,1)}), bf16[16,48,256]{2,1,0:T(8,128)(2,1)S(1)}, u32[]{:S(2)}, u32[]{:S(2)}) async-start(bf16[16,48,256]{2,1,0:T(8,128)(2,1)} %broadcast_in_dim.123), calls=%async_computation | async-start | bytes 786432 | tf_op jit(solution)/shard_map/while/body/eval_jaxpr/all_to_all | solution.py:12
  567.8 17.4 %all-to-all-start.1 = ((bf16[16,48,256]{2,1,0:T(8,128)(2,1)}), bf16[16,48,256]{2,1,0:T(8,128)(2,1)S(1)}, u32[]{:S(2)}, u32[]{:S(2)}) async-start(bf16[16,48,256]{2,1,0:T(8,128)(2,1)} %bitcast.132), calls=%async_computation.1 | async-start | bytes 786432 | tf_op jit(solution)/shard_map/while/body/eval_jaxpr/all_to_all | solution.py:43
  586.6 7.0 collective-permute-start
  595.0 18.3 %all-to-all-start = ((bf16[16,48,256]{2,1,0:T(8,128)(2,1)}), bf16[16,48,256]{2,1,0:T(8,128)(2,1)S(1)}, u32[]{:S(2)}, u32[]{:S(2)}) async-start(bf16[16,48,256]{2,1,0:T(8,128)(2,1)} %broadcast_in_dim.123), calls=%async_computation | async-start | bytes 786432 | tf_op jit(solution)/shard_map/while/body/eval_jaxpr/all_to_all | solution.py:12
  627.1 17.4 %all-to-all-start.1 = ((bf16[16,48,256]{2,1,0:T(8,128)(2,1)}), bf16[16,48,256]{2,1,0:T(8,128)(2,1)S(1)}, u32[]{:S(2)}, u32[]{:S(2)}) async-start(bf16[16,48,256]{2,1,0:T(8,128)(2,1)} %bitcast.132), calls=%async_computation.1 | async-start | bytes 786432 | tf_op jit(solution)/shard_map/while/body/eval_jaxpr/all_to_all | solution.py:43
  645.9 7.0 collective-permute-start
  654.4 18.3 %all-to-all-start = ((bf16[16,48,256]{2,1,0:T(8,128)(2,1)}), bf16[16,48,256]{2,1,0:T(8,128)(2,1)S(1)}, u32[]{:S(2)}, u32[]{:S(2)}) async-start(bf16[16,48,256]{2,1,0:T(8,128)(2,1)} %broadcast_in_dim.123), calls=%async_computation | async-start | bytes 786432 | tf_op jit(solution)/shard_map/while/body/eval_jaxpr/all_to_all | solution.py:12
  686.4 17.4 %all-to-all-start.1 = ((bf16[16,48,256]{2,1,0:T(8,128)(2,1)}), bf16[16,48,256]{2,1,0:T(8,128)(2,1)S(1)}, u32[]{:S(2)}, u32[]{:S(2)}) async-start(bf16[16,48,256]{2,1,0:T(8,128)(2,1)} %bitcast.132), calls=%async_computation.1 | async-start | bytes 786432 | tf_op jit(solution)/shard_map/while/body/eval_jaxpr/all_to_all | solution.py:43
  705.2 7.0 collective-permute-start
  713.7 18.3 %all-to-all-start = ((bf16[16,48,256]{2,1,0:T(8,128)(2,1)}), bf16[16,48,256]{2,1,0:T(8,128)(2,1)S(1)}, u32[]{:S(2)}, u32[]{:S(2)}) async-start(bf16[16,48,256]{2,1,0:T(8,128)(2,1)} %broadcast_in_dim.123), calls=%async_computation | async-start | bytes 786432 | tf_op jit(solution)/shard_map/while/body/eval_jaxpr/all_to_all | solution.py:12
  745.8 17.4 %all-to-all-start.1 = ((bf16[16,48,256]{2,1,0:T(8,128)(2,1)}), bf16[16,48,256]{2,1,0:T(8,128)(2,1)S(1)}, u32[]{:S(2)}, u32[]{:S(2)}) async-start(bf16[16,48,256]{2,1,0:T(8,128)(2,1)} %bitcast.132), calls=%async_computation.1 | async-start | bytes 786432 | tf_op jit(solution)/shard_map/while/body/eval_jaxpr/all_to_all | solution.py:43
  764.6 7.0 collective-permute-start
  773.0 18.3 %all-to-all-start = ((bf16[16,48,256]{2,1,0:T(8,128)(2,1)}), bf16[16,48,256]{2,1,0:T(8,128)(2,1)S(1)}, u32[]{:S(2)}, u32[]{:S(2)}) async-start(bf16[16,48,256]{2,1,0:T(8,128)(2,1)} %broadcast_in_dim.123), calls=%async_computation | async-start | bytes 786432 | tf_op jit(solution)/shard_map/while/body/eval_jaxpr/all_to_all | solution.py:12
  805.1 17.4 %all-to-all-start.1 = ((bf16[16,48,256]{2,1,0:T(8,128)(2,1)}), bf16[16,48,256]{2,1,0:T(8,128)(2,1)S(1)}, u32[]{:S(2)}, u32[]{:S(2)}) async-start(bf16[16,48,256]{2,1,0:T(8,128)(2,1)} %bitcast.132), calls=%async_computation.1 | async-start | bytes 786432 | tf_op jit(solution)/shard_map/while/body/eval_jaxpr/all_to_all | solution.py:43
  823.9 7.0 collective-permute-start
  832.4 18.3 %all-to-all-start = ((bf16[16,48,256]{2,1,0:T(8,128)(2,1)}), bf16[16,48,256]{2,1,0:T(8,128)(2,1)S(1)}, u32[]{:S(2)}, u32[]{:S(2)}) async-start(bf16[16,48,256]{2,1,0:T(8,128)(2,1)} %broadcast_in_dim.123), calls=%async_computation | async-start | bytes 786432 | tf_op jit(solution)/shard_map/while/body/eval_jaxpr/all_to_all | solution.py:12
  864.4 17.4 %all-to-all-start.1 = ((bf16[16,48,256]{2,1,0:T(8,128)(2,1)}), bf16[16,48,256]{2,1,0:T(8,128)(2,1)S(1)}, u32[]{:S(2)}, u32[]{:S(2)}) async-start(bf16[16,48,256]{2,1,0:T(8,128)(2,1)} %bitcast.132), calls=%async_computation.1 | async-start | bytes 786432 | tf_op jit(solution)/shard_map/while/body/eval_jaxpr/all_to_all | solution.py:43
  883.2 7.0 collective-permute-start
  891.7 18.3 %all-to-all-start = ((bf16[16,48,256]{2,1,0:T(8,128)(2,1)}), bf16[16,48,256]{2,1,0:T(8,128)(2,1)S(1)}, u32[]{:S(2)}, u32[]{:S(2)}) async-start(bf16[16,48,256]{2,1,0:T(8,128)(2,1)} %broadcast_in_dim.123), calls=%async_computation | async-start | bytes 786432 | tf_op jit(solution)/shard_map/while/body/eval_jaxpr/all_to_all | solution.py:12
  923.8 17.4 %all-to-all-start.1 = ((bf16[16,48,256]{2,1,0:T(8,128)(2,1)}), bf16[16,48,256]{2,1,0:T(8,128)(2,1)S(1)}, u32[]{:S(2)}, u32[]{:S(2)}) async-start(bf16[16,48,256]{2,1,0:T(8,128)(2,1)} %bitcast.132), calls=%async_computation.1 | async-start | bytes 786432 | tf_op jit(solution)/shard_map/while/body/eval_jaxpr/all_to_all | solution.py:43
  951.0 18.3 %all-to-all-start = ((bf16[16,48,256]{2,1,0:T(8,128)(2,1)}), bf16[16,48,256]{2,1,0:T(8,128)(2,1)S(1)}, u32[]{:S(2)}, u32[]{:S(2)}) async-start(bf16[16,48,256]{2,1,0:T(8,128)(2,1)} %broadcast_in_dim.123), calls=%async_computation | async-start | bytes 786432 | tf_op jit(solution)/shard_map/while/body/eval_jaxpr/all_to_all | solution.py:12
  983.1 17.4 %all-to-all-start.1 = ((bf16[16,48,256]{2,1,0:T(8,128)(2,1)}), bf16[16,48,256]{2,1,0:T(8,128)(2,1)S(1)}, u32[]{:S(2)}, u32[]{:S(2)}) async-start(bf16[16,48,256]{2,1,0:T(8,128)(2,1)} %bitcast.132), calls=%async_computation.1 | async-start | bytes 786432 | tf_op jit(solution)/shard_map/while/body/eval_jaxpr/all_to_all | solution.py:43
  1010.4 18.3 %all-to-all-start = ((bf16[16,48,256]{2,1,0:T(8,128)(2,1)}), bf16[16,48,256]{2,1,0:T(8,128)(2,1)S(1)}, u32[]{:S(2)}, u32[]{:S(2)}) async-start(bf16[16,48,256]{2,1,0:T(8,128)(2,1)} %broadcast_in_dim.123), calls=%async_computation | async-start | bytes 786432 | tf_op jit(solution)/shard_map/while/body/eval_jaxpr/all_to_all | solution.py:12
  1042.5 17.4 %all-to-all-start.1 = ((bf16[16,48,256]{2,1,0:T(8,128)(2,1)}), bf16[16,48,256]{2,1,0:T(8,128)(2,1)S(1)}, u32[]{:S(2)}, u32[]{:S(2)}) async-start(bf16[16,48,256]{2,1,0:T(8,128)(2,1)} %bitcast.132), calls=%async_computation.1 | async-start | bytes 786432 | tf_op jit(solution)/shard_map/while/body/eval_jaxpr/all_to_all | solution.py:43
  1061.2 7.0 collective-permute-start
  1069.7 18.3 %all-to-all-start = ((bf16[16,48,256]{2,1,0:T(8,128)(2,1)}), bf16[16,48,256]{2,1,0:T(8,128)(2,1)S(1)}, u32[]{:S(2)}, u32[]{:S(2)}) async-start(bf16[16,48,256]{2,1,0:T(8,128)(2,1)} %broadcast_in_dim.123), calls=%async_computation | async-start | bytes 786432 | tf_op jit(solution)/shard_map/while/body/eval_jaxpr/all_to_all | solution.py:12
  1101.8 17.4 %all-to-all-start.1 = ((bf16[16,48,256]{2,1,0:T(8,128)(2,1)}), bf16[16,48,256]{2,1,0:T(8,128)(2,1)S(1)}, u32[]{:S(2)}, u32[]{:S(2)}) async-start(bf16[16,48,256]{2,1,0:T(8,128)(2,1)} %bitcast.132), calls=%async_computation.1 | async-start | bytes 786432 | tf_op jit(solution)/shard_map/while/body/eval_jaxpr/all_to_all | solution.py:43
  1120.6 7.0 collective-permute-start
  1129.0 18.3 %all-to-all-start = ((bf16[16,48,256]{2,1,0:T(8,128)(2,1)}), bf16[16,48,256]{2,1,0:T(8,128)(2,1)S(1)}, u32[]{:S(2)}, u32[]{:S(2)}) async-start(bf16[16,48,256]{2,1,0:T(8,128)(2,1)} %broadcast_in_dim.123), calls=%async_computation | async-start | bytes 786432 | tf_op jit(solution)/shard_map/while/body/eval_jaxpr/all_to_all | solution.py:12
  1161.1 17.4 %all-to-all-start.1 = ((bf16[16,48,256]{2,1,0:T(8,128)(2,1)}), bf16[16,48,256]{2,1,0:T(8,128)(2,1)S(1)}, u32[]{:S(2)}, u32[]{:S(2)}) async-start(bf16[16,48,256]{2,1,0:T(8,128)(2,1)} %bitcast.132), calls=%async_computation.1 | async-start | bytes 786432 | tf_op jit(solution)/shard_map/while/body/eval_jaxpr/all_to_all | solution.py:43
  (66 other events, 281.0 us)
Sparse Core Ops, SparseCore 0:
  31.2 41.9 all-gather.3
  76.9 42.9 all-gather.5
where the time goes:
time: 1220 us; the launch traced here: 1190 us
  waiting for transfers between devices  582 us (48%)
  matrix products  177 us (15%)
  starting transfers between devices  159 us (13%)
  local copies, waits for them, and re-layouts  128 us (10%)
  other arithmetic  111 us (9%)
  blocking collectives  20.8 us (2%)
  between operations  13.5 us (1%)
    all_to_all x18, waiting for transfers between devices, summed_on_arrival(): lax.all_to_all(pieces, axis, split_axis=0, concat_axis=0, tiled=True)  226 us
    all_to_all x18, waiting for transfers between devices, from_everyone(): lax.all_to_all(jnp.broadcast_to(array[None], (peers, *array.shape)), axis...  190 us
    ppermute x18, waiting for transfers between devices, shifted(): lax.ppermute(value, axis, [(source, source + steps) for source in range(f...  93 us
    all_to_all x18, starting transfers between devices, from_everyone(): lax.all_to_all(jnp.broadcast_to(array[None], (peers, *array.shape)), axis...  73.5 us
    all_to_all x18, starting transfers between devices, summed_on_arrival(): lax.all_to_all(pieces, axis, split_axis=0, concat_axis=0, tiled=True)  62.1 us
    dot_general x18, matrix products, attention_branch(): key_rows = jnp.dot(normed, w_key, preferred_element_type=jnp.float32)  44.8 us
    dot_general x18, matrix products, attend(): jnp.einsum('hqk,khd->qhd', attn_probs, mixed_values, preferred_element_ty...  40.9 us
    sub x18, matrix products, attend(): expo = jnp.exp(scores - row_top)  40 us
  transfers between devices with their start and end apart: 56, of which 56 were waited for; matrix products, arithmetic and copies ran while one was open for 9% of the time, Pallas kernels for 0%

commit v1 on v0

v1 whole, which is shorter than its diff:
```python
import functools

import jax
import jax.numpy as jnp
import numpy as np
from jax import lax
from jax.experimental import pallas as pl
from jax.experimental.pallas import tpu as pltpu
from jax.sharding import PartitionSpec as P

EPSILON = 1e-05
ROTARY_BASE = 10000.0
CHUNK = 16
MESH = pl.DeviceIdType.MESH
FAR_FIRST = (4, 3, -3, 2, -2, 1, -1, 0)
NEAR_FIRST_GROUPS = ((0, 1, -1), (2, -2), (3, -3), (4,))


def rotary_tables(length, head_dim):
    half = head_dim // 2
    frequency = ROTARY_BASE ** (-(np.arange(half, dtype=np.float32) * 2.0) / head_dim)
    angles = np.arange(length, dtype=np.float32)[:, None] * frequency[None, :].astype(np.float32)
    cosine, sine = np.cos(angles), np.sin(angles)
    return (
        np.concatenate([cosine, cosine], axis=1).astype(np.float32),
        np.concatenate([-sine, sine], axis=1).astype(np.float32),
    )


def kernel(
    sections, peers, length, head_local, head_dim,
    looked, gain_in, mix, cosine, sine, wq_in, wk_in, wv_in, wo_in,
    out,
    blocks, parts, parts_out, emb, fresh, first_values, k_cache, v_cache, gain, wq, wk, wv, wo,
    w_sem, x_sem, p_sem, e_sem, v_sem, xs_sem, ps_sem, es_sem, vs_sem,
):
    chunks, rows, width = looked.shape
    per_sequence = length // rows
    stacks = peers // 2
    s = lax.axis_index("section")
    t = lax.axis_index("tensor")
    z, core = t // 2, lax.rem(t, 2)

    def peer(dz, dc):
        return lax.rem(z + dz + stacks, stacks) * 2 + lax.rem(core + dc, 2)

    def weights():
        pairs = [(wq_in, wq, 0), (wk_in, wk, 1), (wv_in, wv, 2)]
        copies = [pltpu.make_async_copy(a, b, w_sem.at[i]) for a, b, i in pairs]
        for j in range(peers):
            copies.append(
                pltpu.make_async_copy(wo_in.at[0, :, pl.ds(j * width, width)], wo.at[j], w_sem.at[3 + j])
            )
        return copies

    def remote(src, dst, send, recv, section, tensor):
        return pltpu.make_async_remote_copy(
            src_ref=src, dst_ref=dst, send_sem=send, recv_sem=recv,
            device_id=(section, tensor), device_id_type=MESH,
        )

    def await_bytes(ref, sem):
        pltpu.make_async_copy(ref, ref, sem).wait()

    for copy in weights():
        copy.start()

    @pl.when(s != 0)
    def _():
        @pl.loop(0, chunks)
        def _(m):
            remote(looked.at[m], emb.at[m, s], es_sem.at[m], e_sem.at[m], 0, t).start()

    for j in range(peers):
        gain[j] = gain_in[:, j * width : (j + 1) * width].astype(jnp.float32)
    k_cache[...] = jnp.zeros_like(k_cache)
    v_cache[...] = jnp.zeros_like(v_cache)

    def embed(m):
        await_bytes(emb.at[m, pl.ds(1, sections - 1)], e_sem.at[m])
        total = looked[m].astype(jnp.float32)
        for j in range(1, sections):
            total += emb[m, j].astype(jnp.float32)
        blocks[m, t] = total.astype(jnp.bfloat16)
        for dz in FAR_FIRST:
            for dc in (1, 0):
                if (dz, dc) != (0, 0):
                    remote(
                        blocks.at[m, t], blocks.at[m, t], xs_sem.at[m], x_sem.at[m, t], 0, peer(dz, dc)
                    ).start()

    def compute(m):
        q = jnp.zeros((rows, width), jnp.float32)
        k = jnp.zeros((rows, width), jnp.float32)
        v = jnp.zeros((rows, width), jnp.float32)
        squares = jnp.zeros((rows, width), jnp.float32)
        for group in NEAR_FIRST_GROUPS:
            members = [(dz, dc) for dz in group for dc in (0, 1)]
            for dz, dc in members:
                j = peer(dz, dc)
                if (dz, dc) == (0, 0):
                    @pl.when(s != 0)
                    def _():
                        await_bytes(blocks.at[m, t], x_sem.at[m, t])
                else:
                    await_bytes(blocks.at[m, j], x_sem.at[m, j])
            for dz, dc in members:
                j = peer(dz, dc)
                x = blocks[m, j].astype(jnp.float32)
                squares += x * x
                scaled = (x * gain[j]).astype(jnp.bfloat16)
                q += jnp.dot(scaled, wq[j], preferred_element_type=jnp.float32)
                k += jnp.dot(scaled, wk[j], preferred_element_type=jnp.float32)
                v += jnp.dot(scaled, wv[j], preferred_element_type=jnp.float32)
        mean = jnp.sum(squares, axis=-1, keepdims=True) / (peers * width)
        scale = lax.rsqrt(mean + EPSILON)
        q, k, v = q * scale, k * scale, v * scale

        @pl.when(s == 0)
        def _():
            first_values[m] = v.astype(jnp.bfloat16)

        @pl.when(s != 0)
        def _():
            await_bytes(first_values.at[m], v_sem.at[m])

        @pl.when(s != sections - 1)
        def _():
            remote(first_values.at[m], first_values.at[m], vs_sem.at[m], v_sem.at[m], s + 1, t).start()

        source = first_values[m].astype(jnp.float32)
        at = pl.multiple_of(lax.rem(m, per_sequence) * rows, rows)
        cos_rows = cosine[pl.ds(at, rows), :]
        sin_rows = sine[pl.ds(at, rows), :]
        query_at = at + lax.broadcasted_iota(jnp.int32, (rows, length), 0)
        causal = query_at >= lax.broadcasted_iota(jnp.int32, (rows, length), 1)
        heads = []
        for h in range(head_local):
            lanes = slice(h * head_dim, (h + 1) * head_dim)
            qh, kh = q[:, lanes], k[:, lanes]
            qh = (qh * cos_rows + pltpu.roll(qh, head_dim // 2, 1) * sin_rows).astype(jnp.bfloat16)
            kh = (kh * cos_rows + pltpu.roll(kh, head_dim // 2, 1) * sin_rows).astype(jnp.bfloat16)
            rate = mix[0, h]
            vh = (rate * v[:, lanes] + (1.0 - rate) * source[:, lanes]).astype(jnp.bfloat16)
            k_cache[h, pl.ds(at, rows), :] = kh
            v_cache[h, pl.ds(at, rows), :] = vh
            scores = lax.dot_general(
                qh, k_cache[h], (((1,), (1,)), ((), ())), preferred_element_type=jnp.float32
            ) * head_dim ** (-0.5)
            scores = jnp.where(causal, scores, -1e30)
            expo = jnp.exp(scores - jnp.max(scores, axis=-1, keepdims=True))
            probs = (expo / jnp.sum(expo, axis=-1, keepdims=True)).astype(jnp.bfloat16)
            heads.append(jnp.dot(probs, v_cache[h], preferred_element_type=jnp.float32))
        attended = jnp.concatenate(heads, axis=1).astype(jnp.bfloat16)
        for dz in FAR_FIRST:
            for dc in (1, 0):
                j = peer(dz, dc)
                part = jnp.dot(attended, wo[j], preferred_element_type=jnp.float32).astype(jnp.bfloat16)
                if (dz, dc) == (0, 0):
                    parts[m, t] = part
                else:
                    parts_out[m, j] = part
                    remote(
                        parts_out.at[m, j], parts.at[m, t], ps_sem.at[m], p_sem.at[m], s, j
                    ).start()

    def reduce(m):
        await_bytes(parts.at[m, pl.ds(1, peers - 1)], p_sem.at[m])
        total = parts[m, 0].astype(jnp.float32)
        for j in range(1, peers):
            total += parts[m, j].astype(jnp.float32)
        hidden = (blocks[m, t].astype(jnp.float32) + total).astype(jnp.bfloat16)
        out[m] = hidden

        @pl.when(s != sections - 1)
        def _():
            fresh[m] = hidden
            for dz in FAR_FIRST:
                for dc in (1, 0):
                    remote(
                        fresh.at[m], blocks.at[m, t], xs_sem.at[m], x_sem.at[m, t], s + 1, peer(dz, dc)
                    ).start()

    @pl.when(s == 0)
    def _():
        embed(0)

    for copy in weights():
        copy.wait()

    @pl.loop(0, chunks)
    def _(i):
        @pl.when((s == 0) & (i + 1 < chunks))
        def _():
            embed(i + 1)

        compute(i)

        @pl.when(i >= 1)
        def _():
            reduce(i - 1)

    reduce(chunks - 1)

    @pl.loop(0, chunks)
    def _(m):
        await_bytes(parts_out.at[m, pl.ds(1, peers - 1)], ps_sem.at[m])

        @pl.when(s != 0)
        def _():
            await_bytes(looked.at[m], es_sem.at[m])

        @pl.when(s == 0)
        def _():
            await_bytes(blocks.at[m, pl.ds(1, peers - 1)], xs_sem.at[m])

        @pl.when(s != sections - 1)
        def _():
            await_bytes(first_values.at[m], vs_sem.at[m])
            await_bytes(blocks.at[m], xs_sem.at[m])


def shards(
    token_ids, emb_table, attn_gain, query_weight, key_weight, value_weight, mix_weight, out_weight
):
    section_rank = lax.axis_index("section")
    sections, peers = lax.axis_size("section"), lax.axis_size("tensor")
    batches, length = token_ids.shape
    vocab_local, width = emb_table.shape
    head_local = mix_weight.shape[1]
    head_dim = query_weight.shape[2] // head_local
    chunks = batches * length // CHUNK
    flat_ids = token_ids.reshape(-1) - section_rank * vocab_local
    one_hot = (flat_ids[:, None] == jnp.arange(vocab_local, dtype=jnp.int32)[None, :]).astype(
        jnp.bfloat16
    )
    looked = jnp.dot(one_hot, emb_table, preferred_element_type=jnp.float32)
    looked = looked.astype(jnp.bfloat16).reshape(chunks, CHUNK, width)
    cosine, sine = rotary_tables(length, head_dim)
    tiles = (peers, width, width)
    vmem, anywhere = pl.BlockSpec(memory_space=pltpu.VMEM), pl.BlockSpec(memory_space=pl.ANY)
    bf16, dma = jnp.bfloat16, pltpu.SemaphoreType.DMA
    result = pl.pallas_call(
        functools.partial(kernel, sections, peers, length, head_local, head_dim),
        out_shape=jax.ShapeDtypeStruct((chunks, CHUNK, width), bf16),
        in_specs=[vmem, vmem, pl.BlockSpec(memory_space=pltpu.SMEM), vmem, vmem] + [anywhere] * 4,
        out_specs=vmem,
        scratch_shapes=[
            pltpu.VMEM((chunks, peers, CHUNK, width), bf16),
            pltpu.VMEM((chunks, peers, CHUNK, width), bf16),
            pltpu.VMEM((chunks, peers, CHUNK, width), bf16),
            pltpu.VMEM((chunks, sections, CHUNK, width), bf16),
            pltpu.VMEM((chunks, CHUNK, width), bf16),
            pltpu.VMEM((chunks, CHUNK, width), bf16),
            pltpu.VMEM((head_local, length, head_dim), bf16),
            pltpu.VMEM((head_local, length, head_dim), bf16),
            pltpu.VMEM((peers, 1, width), jnp.float32),
            pltpu.VMEM(tiles, bf16),
            pltpu.VMEM(tiles, bf16),
            pltpu.VMEM(tiles, bf16),
            pltpu.VMEM(tiles, bf16),
            dma((3 + peers,)),
            dma((chunks, peers)),
            dma((chunks,)),
            dma((chunks,)),
            dma((chunks,)),
            dma((chunks,)),
            dma((chunks,)),
            dma((chunks,)),
            dma((chunks,)),
        ],
        compiler_params=pltpu.CompilerParams(has_side_effects=True, vmem_limit_bytes=40 * 2**20),
        name="relay",
    )(
        looked, attn_gain, mix_weight, jnp.asarray(cosine), jnp.asarray(sine),
        query_weight.reshape(tiles), key_weight.reshape(tiles), value_weight.reshape(tiles), out_weight,
    )
    return result.reshape(1, batches, length, width)


def solution(mesh):
    in_specs = (
        P(),
        P("section", "tensor"),
        P("section", None),
        P("section", None, "tensor"),
        P("section", None, "tensor"),
        P("section", None, "tensor"),
        P("section", "tensor"),
        P("section", "tensor", None),
    )
    out_specs = P("section", None, None, "tensor")
    return jax.shard_map(shards, mesh=mesh, in_specs=in_specs, out_specs=out_specs, check_vma=False)
```

time: 1220 us -> 381 us (0.31); the launches traced: 1190 us -> 380 us
  waiting for transfers between devices: 582 us -> 0 us
  Pallas kernels: 0 us -> 369 us
  matrix products: 177 us -> 0.37 us
  starting transfers between devices: 159 us -> 0 us
  local copies, waits for them, and re-layouts: 128 us -> 10.3 us
  other arithmetic: 111 us -> 0.77 us
  blocking collectives: 20.8 us -> 0 us
  between operations: 13.5 us -> 0.03 us
    all_to_all x36 -> x0, waiting for transfers between devices: 416 us -> none  [the longest x18 226 us: summed_on_arrival(): lax.all_to_all(pieces, axis, split_axis=0, concat_axis=0, tiled=True)]
    pallas_call x0 -> x1, Pallas kernels: none -> 369 us  [shards(): pl.pallas_call(functools.partial(kernel, sections, peers, length, head_lo...]
    dot_general x72 -> x0, matrix products: 137 us -> none  [the longest x18 44.8 us: attention_branch(): key_rows = jnp.dot(normed, w_key, preferred_element_type=jnp.float32)]
    all_to_all x36 -> x0, starting transfers between devices: 136 us -> none  [the longest x18 73.5 us: from_everyone(): lax.all_to_all(jnp.broadcast_to(array[None], (peers, *array.shape)), axis...]
    ppermute x18 -> x0, waiting for transfers between devices: 93 us -> none  [shifted(): lax.ppermute(value, axis, [(source, source + steps) for source in range(f...]
    all_gather x2 -> x0, waiting for transfers between devices: 73.9 us -> none  [the longest x1 39 us: shards(): first_full = lax.all_gather(first_shard, 'tensor', axis=1, tiled=True)]
    dynamic_slice x37 -> x0, local copies, waits for them, and re-layouts: 49.7 us -> none  [the longest x18 24.5 us: attention_branch(): lax.dynamic_index_in_dim(source_values, micro_index, 0, keepdims=False)]
    sub x18 -> x0, matrix products: 40 us -> none  [attend(): expo = jnp.exp(scores - row_top)]
  transfers between devices with their start and end apart: 56 -> 0, of which waited for: 56 -> 0; matrix products, arithmetic and copies ran while one was open for 9% -> 0% of each run, Pallas kernels for 0% -> 0%
where the time goes in v1:
time: 381 us; the launch traced here: 380 us
  Pallas kernels  369 us (97%)
  local copies, waits for them, and re-layouts  10.3 us (3%)
    pallas_call x1, Pallas kernels, shards(): pl.pallas_call(functools.partial(kernel, sections, peers, length, head_lo...  369 us
    unnamed x19, local copies, waits for them, and re-layouts  10.2 us

profile of v1, /device:TPU:31, one launch (start us, length us, event | category | flops | bytes accessed | tf_op | source)
XLA Modules:
  0.0 380.1 jit_solution(2441932309132498085)
XLA Ops:
  0.0 0.0 copy-start
  0.0 0.8 broadcast_subtract_fusion
  0.8 0.1 sub.15
  0.9 0.4 copy-done
  1.2 0.4 fusion.1
  1.6 0.0 copy-start.1
  1.6 1.6 copy-done.1
  3.2 0.0 copy-start.2
  3.2 1.6 copy-done.2
  4.8 0.0 copy-start.3
  4.8 1.6 copy-done.3
  6.4 0.0 copy-start.4
  6.4 1.6 copy-done.4
  8.0 0.0 copy-start.5
  8.0 0.7 copy-done.5
  8.7 0.0 copy-start.6
  8.7 0.7 copy-done.6
  9.5 0.0 copy-start.7
  9.5 0.7 copy-done.7
  10.2 0.0 copy-start.8
  10.2 0.7 copy-done.8
  10.8 368.7 %relay.1 = bf16[9,16,256]{2,1,0:T(8,128)(2,1)S(1)} custom-call(bf16[9,16,256]{2,1,0:T(8,128)(2,1)S(1)} %bitcast.10, bf16[1,4096]{1,0:T(2,128)(2,1)S(1)} %copy-done.7, f32[1,2]{1,0:T(1,128)S(1)} %copy-done.8, f32[48,128]{1,0:T(8,128)S(1)} %copy-done.6, f32[48,128]{1,0:T(8,128)S(1)} %copy-done.5, bf16[16,256,256]{2,1,0:T(8,128)(2,1)S(1)} %bitcast.6, ...), custom_call_target="tpu_custom_call" | custom-call | tf_op jit(solution)/shard_map/relay/pallas_call | solution.py:243
  379.5 0.6 copy.12
Async XLA Ops:
  0.0 1.2 copy-start
  1.6 1.6 copy-start.1
  3.2 1.6 copy-start.2
  4.8 1.6 copy-start.3
  6.4 1.6 copy-start.4
  8.0 0.7 copy-start.5
  8.7 0.7 copy-start.6
  9.5 0.7 copy-start.7
  10.2 0.7 copy-start.8
